TPU v7x, 32 devices: a whole 2x2x4 slice. The times are simulated.
32 devices in a mesh: seq: 8 (over z, core), ctx: 4 (over y, x).
Axes of the slice: x: 2, y: 2, z: 4, core: 2. Of those that a mesh axis runs over, the one named last changes fastest.
Arguments:
- queries: bfloat16 [8192, 2048], P(('seq', 'ctx')), parts along dimension 0, may hold values from -16 to 16
- key_rows: bfloat16 [8192, 512], P(('seq', 'ctx')), parts along dimension 0, may hold values from -16 to 16
- value_rows: bfloat16 [8192, 512], P(('seq', 'ctx')), parts along dimension 0, may hold values from -6 to 6
- doc_lengths: int32 [32], P('seq'), parts along dimension 0, may hold values from 1 to 512, 1024 in all
- block_owner: int32 [64], P('seq'), parts along dimension 0, may hold values from 0 to 7, as said below
Outputs:
- attended: bfloat16 [8192, 2048], P(('seq', 'ctx')), parts along dimension 0
There are 8 independent parts, one for each index of `seq`. A program takes and returns all parts, laid end to end along the dimension named above; each array names one. Nothing has to cross between parts.
Inputs may be any that keep to these rules, and one draw needn't show every extreme that they name: `block_owner`: slots come in aligned groups of 4 blocks; each group holds exactly the blocks with the same group number, in some order.
All inputs are finite; a program needn't handle non-finite values.
Results may differ from a plain program's by a relative error of at most 0.0035.
Values may be sent and summed in bfloat16 or wider, within the bound.
A program may use at most 64 MiB of HBM per device.

v0:
```python
import functools
import math

import jax
import jax.numpy as jnp
from jax import lax
from jax.experimental import pallas as pl
from jax.experimental.pallas import tpu as pltpu
from jax.sharding import PartitionSpec as P

HEAD_DIM = 128
BLOCK_ROWS = 128
GROUP_SIZE = 4
NEGATIVE = -1e30
MESH = pl.DeviceIdType.MESH
EXPONENT = HEAD_DIM ** -0.5 * math.log2(math.e)

OWN, PARTNER, PREV, CROSS = range(4)


def kernel(
    devices, q_hbm, k_hbm, v_hbm, lengths, owner, out,
    q, kbuf, vbuf, bias, scores, top, weights, total, acc,
    local_sem, send_sem, recv_sem,
):
    rows = q.shape[0]
    kv_heads = kbuf.shape[2] // HEAD_DIM
    half = rows // 2
    me = lax.axis_index("ctx")
    partner = me + 1 - 2 * (me % 2)
    prev = me - 2
    cross = partner - 2
    nxt = me + 2
    has_prev = me >= 2
    has_next = me < devices - 2

    local = [
        pltpu.make_async_copy(k_hbm, kbuf.at[OWN], local_sem.at[0]),
        pltpu.make_async_copy(q_hbm, q, local_sem.at[1]),
        pltpu.make_async_copy(v_hbm, vbuf.at[OWN], local_sem.at[2]),
    ]
    for copy in local:
        copy.start()

    barrier = pltpu.get_barrier_semaphore()

    def greet(device):
        pl.semaphore_signal(barrier, inc=1, device_id={"ctx": device}, device_id_type=MESH)

    greet(partner)
    pl.when(has_prev)(lambda: greet(prev))
    pl.when(has_next)(lambda: greet(nxt))
    pl.semaphore_wait(barrier, 1 + has_prev.astype(jnp.int32) + has_next.astype(jnp.int32))

    def column(head):
        return pl.ds(head * HEAD_DIM if isinstance(head, int) else pl.multiple_of(head * HEAD_DIM, HEAD_DIM), HEAD_DIM)

    part = [pl.ds(0, half), pl.ds(half, half)]

    def remote(source, target, index, device):
        return pltpu.make_async_remote_copy(
            src_ref=source, dst_ref=target, send_sem=send_sem.at[index],
            recv_sem=recv_sem.at[index], device_id={"ctx": device}, device_id_type=MESH,
        )

    def own_copy(hbm, buf, piece, chunk, index, device):
        return remote(buf.at[OWN, part[piece]], buf.at[chunk, part[piece]], index, device)

    def relay(buf, chunk, piece, index, device):
        return remote(buf.at[chunk, part[piece]], buf.at[CROSS, part[piece]], index, device)

    k_partner = [own_copy(k_hbm, kbuf, i, PARTNER, i, partner) for i in (0, 1)]
    v_partner = [own_copy(v_hbm, vbuf, i, PARTNER, 2 + i, partner) for i in (0, 1)]
    k_next = [own_copy(k_hbm, kbuf, i, PREV, 4 + i, nxt) for i in (0, 1)]
    v_next = [own_copy(v_hbm, vbuf, i, PREV, 6 + i, nxt) for i in (0, 1)]
    k_to_next = relay(kbuf, PARTNER, 1, 8, nxt)
    k_to_partner = relay(kbuf, PREV, 0, 9, partner)

    def relay_values(chunk, piece, g, index, device):
        view = part[piece], column(g)
        return remote(vbuf.at[(chunk, *view)], vbuf.at[(CROSS, *view)], index + g, device)

    def v_to_next(g):
        return relay_values(PARTNER, 1, g, 10, nxt)

    def v_to_partner(g):
        return relay_values(PREV, 0, g, 10 + kv_heads, partner)

    def start_all(copy_of):
        for g in range(kv_heads):
            copy_of(g).start()

    def start_both(copies):
        copies[0].start()
        copies[1].start()

    local[0].wait()
    k_partner[1].start()
    pl.when(has_next)(lambda: k_next[0].start())
    k_partner[0].start()
    pl.when(has_next)(lambda: k_next[1].start())

    down = lax.broadcasted_iota(jnp.int32, (half, 1), 0)
    along = lax.broadcasted_iota(jnp.int32, (1, half), 1)

    def mask(chunk, device):
        for i in range(2):
            places = owner[2 * me + i] * BLOCK_ROWS + down
            end = lengths[0]
            starts = jnp.where(places >= end, end, 0)
            for d in range(1, lengths.shape[0]):
                end = end + lengths[d]
                starts = jnp.where(places >= end, end, starts)
            for j in range(2):
                keys = owner[2 * device + j] * BLOCK_ROWS + along
                allowed = (keys >= starts) & (keys <= places)
                bias[chunk, pl.ds(i * half, half), pl.ds(j * half, half)] = jnp.where(
                    allowed, 0.0, NEGATIVE
                )

    mask(OWN, me)
    mask(PARTNER, partner)

    @pl.when(has_prev)
    def _():
        mask(PREV, prev)
        mask(CROSS, cross)

    def score(chunk):
        @pl.loop(0, kv_heads, unroll=True)
        def _(g):
            keys = kbuf[chunk, :, column(g)]
            for j in range(GROUP_SIZE):
                h = g * GROUP_SIZE + j
                s = lax.dot_general(
                    q[:, column(h)], keys, (((1,), (1,)), ((), ())),
                    preferred_element_type=jnp.float32,
                )
                s = s + bias[chunk]
                scores[h, chunk] = s
                best = jnp.maximum(s[:, :half], s[:, half:])
                if chunk != OWN:
                    best = jnp.maximum(best, top[h])
                top[h] = best

    def weigh(first, last, chunks):
        @pl.loop(first, last, unroll=True)
        def _(g):
            values = vbuf[OWN, :, column(g)]
            for j in range(GROUP_SIZE):
                h = g * GROUP_SIZE + j
                largest = jnp.max(top[h], axis=1, keepdims=True)
                summed = jnp.zeros((rows, half), jnp.float32)
                for c in range(chunks):
                    w = jnp.exp2((scores[h, c] - largest) * EXPONENT)
                    summed = summed + (w[:, :half] + w[:, half:])
                    weights[h, c] = w.astype(jnp.bfloat16)
                total[h] = jnp.sum(summed, axis=1, keepdims=True)
                acc[h] = jnp.dot(weights[h, OWN], values, preferred_element_type=jnp.float32)

    def mix(chunk):
        @pl.loop(0, kv_heads, unroll=True)
        def _(g):
            values = vbuf[chunk, :, column(g)]
            for j in range(GROUP_SIZE):
                h = g * GROUP_SIZE + j
                acc[h] += jnp.dot(weights[h, chunk], values, preferred_element_type=jnp.float32)

    def finish(chunk):
        @pl.loop(0, kv_heads, unroll=True)
        def _(g):
            if chunk == CROSS:
                v_to_next(g).wait_recv()
                v_to_partner(g).wait_recv()
            values = vbuf[chunk, :, column(g)]
            for j in range(GROUP_SIZE):
                h = g * GROUP_SIZE + j
                mixed = acc[h] + jnp.dot(
                    weights[h, chunk], values, preferred_element_type=jnp.float32
                )
                out[:, column(h)] = (mixed * (1.0 / total[h])).astype(jnp.bfloat16)

    k_partner[1].wait_recv()
    pl.when(has_next)(k_to_next.start)

    @pl.when(has_prev)
    def _():
        k_next[0].wait_recv()
        k_to_partner.start()

    local[2].wait()
    v_partner[1].start()
    v_partner[0].start()
    pl.when(has_next)(lambda: start_both(v_next))
    local[1].wait()
    score(OWN)
    k_partner[0].wait_recv()
    score(PARTNER)

    @pl.when(has_prev)
    def _():
        k_next[1].wait_recv()
        score(PREV)
        k_to_next.wait_recv()
        k_to_partner.wait_recv()
        score(CROSS)

    middle = kv_heads // 2
    pl.when(has_prev)(lambda: weigh(0, middle, 4))
    pl.when(jnp.logical_not(has_prev))(lambda: weigh(0, middle, 2))
    v_partner[1].wait_recv()
    pl.when(has_next)(lambda: start_all(v_to_next))

    @pl.when(has_prev)
    def _():
        v_next[0].wait_recv()
        start_all(v_to_partner)
        weigh(middle, kv_heads, 4)

    pl.when(jnp.logical_not(has_prev))(lambda: weigh(middle, kv_heads, 2))
    v_partner[0].wait_recv()

    @pl.when(has_prev)
    def _():
        mix(PARTNER)
        v_next[1].wait_recv()
        mix(PREV)
        finish(CROSS)

    pl.when(jnp.logical_not(has_prev))(lambda: finish(PARTNER))

    for copy in k_partner + v_partner:
        copy.wait_send()

    @pl.when(has_next)
    def _():
        for copy in k_next + v_next + [k_to_next] + [v_to_next(g) for g in range(kv_heads)]:
            copy.wait_send()

    @pl.when(has_prev)
    def _():
        for copy in [k_to_partner] + [v_to_partner(g) for g in range(kv_heads)]:
            copy.wait_send()


def body(devices, queries, key_rows, value_rows, doc_lengths, block_owner):
    rows, width = queries.shape
    kv_width = key_rows.shape[1]
    heads, kv_heads = width // HEAD_DIM, kv_width // HEAD_DIM
    half = rows // 2
    return pl.pallas_call(
        functools.partial(kernel, devices),
        out_shape=pltpu.VMEM((rows, width), jnp.bfloat16),
        in_specs=[pl.BlockSpec(memory_space=pl.ANY)] * 3
        + [pl.BlockSpec(memory_space=pltpu.SMEM)] * 2,
        out_specs=pl.BlockSpec(memory_space=pltpu.VMEM),
        scratch_shapes=[
            pltpu.VMEM((rows, width), jnp.bfloat16),
            pltpu.VMEM((4, rows, kv_width), jnp.bfloat16),
            pltpu.VMEM((4, rows, kv_width), jnp.bfloat16),
            pltpu.VMEM((4, rows, rows), jnp.float32),
            pltpu.VMEM((heads, 4, rows, rows), jnp.float32),
            pltpu.VMEM((heads, rows, half), jnp.float32),
            pltpu.VMEM((heads, 4, rows, rows), jnp.bfloat16),
            pltpu.VMEM((heads, rows, 1), jnp.float32),
            pltpu.VMEM((heads, rows, HEAD_DIM), jnp.float32),
            pltpu.SemaphoreType.DMA((3,)),
            pltpu.SemaphoreType.DMA((10 + 2 * kv_heads,)),
            pltpu.SemaphoreType.DMA((10 + 2 * kv_heads,)),
        ],
        compiler_params=pltpu.CompilerParams(
            collective_id=0, has_side_effects=True, vmem_limit_bytes=56 * 1024 * 1024
        ),
        name="attend",
    )(queries, key_rows, value_rows, doc_lengths, block_owner)


def solution(mesh):
    rows = P(("seq", "ctx"), None)
    return jax.shard_map(
        functools.partial(body, mesh.shape["ctx"]),
        mesh=mesh,
        in_specs=(rows, rows, rows, P("seq"), P("seq")),
        out_specs=rows,
        check_vma=False,
    )
```

profile of v0, /device:TPU:28, one launch (start us, length us, event | category | flops | bytes accessed | tf_op | source)
XLA Modules:
  0.0 22.6 jit_solution(5654670408901016910)
XLA Ops:
  0.0 21.7 %attend.1 = bf16[256,2048]{1,0:T(8,128)(2,1)S(1)} custom-call(bf16[256,2048]{1,0:T(8,128)(2,1)} %q_hbm.1, bf16[256,512]{1,0:T(8,128)(2,1)} %k_hbm.1, bf16[256,512]{1,0:T(8,128)(2,1)} %v_hbm.1, s32[4]{0:T(128)} %lengths.1, s32[8]{0:T(128)} %owner.1), custom_call_target="tpu_custom_call" | custom-call | tf_op jit(solution)/shard_map/attend/pallas_call | solution.py:251
  21.7 1.0 %copy.7 = bf16[256,2048]{1,0:T(8,128)(2,1)} copy(bf16[256,2048]{1,0:T(8,128)(2,1)S(1)} %attend.1) | data formatting | bytes 2097152
where the time goes:
time: 22.8 us; the launch traced here: 22.6 us
  Pallas kernels  21.7 us (95%)
  local copies, waits for them, and re-layouts  0.97 us (4%)
    pallas_call x1, Pallas kernels, body(): pl.pallas_call(functools.partial(kernel, devices), out_shape=pltpu.VMEM((...  21.7 us
    unnamed x1, local copies, waits for them, and re-layouts  0.97 us

commit v1 on v0

v1 whole, which is shorter than its diff:
```python
import functools
import math

import jax
import jax.numpy as jnp
from jax import lax
from jax.experimental import pallas as pl
from jax.experimental.pallas import tpu as pltpu
from jax.sharding import PartitionSpec as P

HEAD_DIM = 128
BLOCK_ROWS = 128
GROUP_SIZE = 4
NEGATIVE = -1e30
MESH = pl.DeviceIdType.MESH
EXPONENT = HEAD_DIM ** -0.5 * math.log2(math.e)

OWN, PARTNER, PREV, CROSS = range(4)


def kernel(
    devices, q_hbm, k_hbm, v_hbm, lengths_hbm, owner_hbm, out,
    lengths, owner, q, kbuf, vbuf, bias, scores, top, weights, total, acc,
    local_sem, send_sem, recv_sem,
):
    rows = q.shape[0]
    kv_heads = kbuf.shape[2] // HEAD_DIM
    half = rows // 2
    me = lax.axis_index("ctx")
    partner = me + 1 - 2 * (me % 2)
    prev = me - 2
    cross = partner - 2
    nxt = me + 2
    has_prev = me >= 2
    has_next = me < devices - 2

    barrier = pltpu.get_barrier_semaphore()

    def greet(device):
        pl.semaphore_signal(barrier, inc=1, device_id={"ctx": device}, device_id_type=MESH)

    greet(partner)
    pl.when(has_prev)(lambda: greet(prev))
    pl.when(has_next)(lambda: greet(nxt))

    local = [
        pltpu.make_async_copy(k_hbm, kbuf.at[OWN], local_sem.at[0]),
        pltpu.make_async_copy(v_hbm, vbuf.at[OWN], local_sem.at[1]),
        pltpu.make_async_copy(lengths_hbm, lengths, local_sem.at[2]),
        pltpu.make_async_copy(owner_hbm, owner, local_sem.at[3]),
        pltpu.make_async_copy(q_hbm, q, local_sem.at[4]),
    ]
    for copy in local:
        copy.start()
    pl.semaphore_wait(barrier, 1 + has_prev.astype(jnp.int32) + has_next.astype(jnp.int32))

    def column(head):
        return pl.ds(head * HEAD_DIM if isinstance(head, int) else pl.multiple_of(head * HEAD_DIM, HEAD_DIM), HEAD_DIM)

    part = [pl.ds(0, half), pl.ds(half, half)]

    def remote(source, target, index, device):
        return pltpu.make_async_remote_copy(
            src_ref=source, dst_ref=target, send_sem=send_sem.at[index],
            recv_sem=recv_sem.at[index], device_id={"ctx": device}, device_id_type=MESH,
        )

    def own_copy(hbm, buf, piece, chunk, index, device):
        return remote(hbm.at[part[piece]], buf.at[chunk, part[piece]], index, device)

    def relay(buf, chunk, piece, index, device):
        return remote(buf.at[chunk, part[piece]], buf.at[CROSS, part[piece]], index, device)

    k_partner = [own_copy(k_hbm, kbuf, i, PARTNER, i, partner) for i in (0, 1)]
    k_next = [own_copy(k_hbm, kbuf, i, PREV, 2 + i, nxt) for i in (0, 1)]
    k_to_next = relay(kbuf, PARTNER, 1, 4, nxt)
    k_to_partner = relay(kbuf, PREV, 0, 5, partner)
    v_first_partner = own_copy(v_hbm, vbuf, 1, PARTNER, 6, partner)
    v_first_next = own_copy(v_hbm, vbuf, 0, PREV, 7, nxt)

    def own_values(chunk, piece, g, index, device):
        view = part[piece], column(g)
        return remote(v_hbm.at[view], vbuf.at[(chunk, *view)], index + g, device)

    def relay_values(chunk, piece, g, index, device):
        view = part[piece], column(g)
        return remote(vbuf.at[(chunk, *view)], vbuf.at[(CROSS, *view)], index + g, device)

    def v_partner(g):
        return own_values(PARTNER, 0, g, 8, partner)

    def v_next(g):
        return own_values(PREV, 1, g, 8 + kv_heads, nxt)

    def v_to_next(g):
        return relay_values(PARTNER, 1, g, 8 + 2 * kv_heads, nxt)

    def v_to_partner(g):
        return relay_values(PREV, 0, g, 8 + 3 * kv_heads, partner)

    def start_all(copy_of):
        for g in range(kv_heads):
            copy_of(g).start()

    k_partner[1].start()
    pl.when(has_next)(lambda: k_next[0].start())
    k_partner[0].start()
    pl.when(has_next)(lambda: k_next[1].start())

    local[2].wait()
    local[3].wait()
    down = lax.broadcasted_iota(jnp.int32, (half, 1), 0)
    along = lax.broadcasted_iota(jnp.int32, (1, half), 1)

    def mask(chunk, device):
        for i in range(2):
            places = owner[2 * me + i] * BLOCK_ROWS + down
            end = lengths[0]
            starts = jnp.where(places >= end, end, 0)
            for d in range(1, lengths.shape[0]):
                end = end + lengths[d]
                starts = jnp.where(places >= end, end, starts)
            for j in range(2):
                keys = owner[2 * device + j] * BLOCK_ROWS + along
                allowed = (keys >= starts) & (keys <= places)
                bias[chunk, pl.ds(i * half, half), pl.ds(j * half, half)] = jnp.where(
                    allowed, 0.0, NEGATIVE
                )

    mask(OWN, me)
    mask(PARTNER, partner)

    @pl.when(has_prev)
    def _():
        mask(PREV, prev)
        mask(CROSS, cross)

    def score(chunk):
        @pl.loop(0, kv_heads, unroll=True)
        def _(g):
            keys = kbuf[chunk, :, column(g)]
            for j in range(GROUP_SIZE):
                h = g * GROUP_SIZE + j
                s = lax.dot_general(
                    q[:, column(h)], keys, (((1,), (1,)), ((), ())),
                    preferred_element_type=jnp.float32,
                )
                s = s + bias[chunk]
                scores[h, chunk] = s
                best = jnp.maximum(s[:, :half], s[:, half:])
                if chunk != OWN:
                    best = jnp.maximum(best, top[h])
                top[h] = best

    def weigh(g, chunks):
        own = vbuf[OWN, :, column(g)]
        for j in range(GROUP_SIZE):
            h = g * GROUP_SIZE + j
            largest = jnp.max(top[h], axis=1, keepdims=True)
            summed = jnp.zeros((rows, half), jnp.float32)
            for c in range(chunks):
                w = jnp.exp2((scores[h, c] - largest) * EXPONENT)
                summed = summed + (w[:, :half] + w[:, half:])
                weights[h, c] = w.astype(jnp.bfloat16)
            total[h] = jnp.sum(summed, axis=1, keepdims=True)
            acc[h] = jnp.dot(weights[h, OWN], own, preferred_element_type=jnp.float32)

    def mix(g):
        partners = vbuf[PARTNER, :, column(g)]
        prevs = vbuf[PREV, :, column(g)]
        for j in range(GROUP_SIZE):
            h = g * GROUP_SIZE + j
            acc[h] += jnp.dot(
                weights[h, PARTNER], partners, preferred_element_type=jnp.float32
            ) + jnp.dot(weights[h, PREV], prevs, preferred_element_type=jnp.float32)

    def finish(chunk):
        @pl.loop(0, kv_heads, unroll=True)
        def _(g):
            if chunk == CROSS:
                v_to_next(g).wait_recv()
                v_to_partner(g).wait_recv()
            values = vbuf[chunk, :, column(g)]
            for j in range(GROUP_SIZE):
                h = g * GROUP_SIZE + j
                mixed = acc[h] + jnp.dot(
                    weights[h, chunk], values, preferred_element_type=jnp.float32
                )
                out[:, column(h)] = (mixed * (1.0 / total[h])).astype(jnp.bfloat16)

    k_partner[1].wait_recv()
    pl.when(has_next)(k_to_next.start)

    @pl.when(has_prev)
    def _():
        k_next[0].wait_recv()
        k_to_partner.start()

    v_first_partner.start()

    @pl.when(has_next)
    def _():
        v_first_next.start()
        start_all(v_next)

    start_all(v_partner)
    local[0].wait()
    local[4].wait()
    score(OWN)
    k_partner[0].wait_recv()
    score(PARTNER)

    @pl.when(has_prev)
    def _():
        k_next[1].wait_recv()
        score(PREV)
        k_to_next.wait_recv()
        k_to_partner.wait_recv()
        score(CROSS)

    local[1].wait()
    middle = kv_heads // 2

    def weigh_all(first, last):
        for g in range(first, last):
            pl.when(has_prev)(lambda: weigh(g, 4))
            pl.when(jnp.logical_not(has_prev))(lambda: weigh(g, 2))

    weigh_all(0, middle)
    v_first_partner.wait_recv()
    pl.when(has_next)(lambda: start_all(v_to_next))

    @pl.when(has_prev)
    def _():
        v_first_next.wait_recv()
        start_all(v_to_partner)

    weigh_all(middle, kv_heads)
    for g in range(kv_heads):
        v_partner(g).wait_recv()

        @pl.when(has_prev)
        def _():
            v_next(g).wait_recv()
            mix(g)

    pl.when(has_prev)(lambda: finish(CROSS))
    pl.when(jnp.logical_not(has_prev))(lambda: finish(PARTNER))

    for copy in k_partner + [v_first_partner] + [v_partner(g) for g in range(kv_heads)]:
        copy.wait_send()

    @pl.when(has_next)
    def _():
        for copy in k_next + [k_to_next, v_first_next]:
            copy.wait_send()
        for g in range(kv_heads):
            v_next(g).wait_send()
            v_to_next(g).wait_send()

    @pl.when(has_prev)
    def _():
        k_to_partner.wait_send()
        for g in range(kv_heads):
            v_to_partner(g).wait_send()


def body(devices, queries, key_rows, value_rows, doc_lengths, block_owner):
    rows, width = queries.shape
    kv_width = key_rows.shape[1]
    heads, kv_heads = width // HEAD_DIM, kv_width // HEAD_DIM
    half = rows // 2
    return pl.pallas_call(
        functools.partial(kernel, devices),
        out_shape=pltpu.VMEM((rows, width), jnp.bfloat16),
        in_specs=[pl.BlockSpec(memory_space=pl.ANY)] * 5,
        out_specs=pl.BlockSpec(memory_space=pltpu.VMEM),
        scratch_shapes=[
            pltpu.SMEM(doc_lengths.shape, jnp.int32),
            pltpu.SMEM(block_owner.shape, jnp.int32),
            pltpu.VMEM((rows, width), jnp.bfloat16),
            pltpu.VMEM((4, rows, kv_width), jnp.bfloat16),
            pltpu.VMEM((4, rows, kv_width), jnp.bfloat16),
            pltpu.VMEM((4, rows, rows), jnp.float32),
            pltpu.VMEM((heads, 4, rows, rows), jnp.float32),
            pltpu.VMEM((heads, rows, half), jnp.float32),
            pltpu.VMEM((heads, 4, rows, rows), jnp.bfloat16),
            pltpu.VMEM((heads, rows, 1), jnp.float32),
            pltpu.VMEM((heads, rows, HEAD_DIM), jnp.float32),
            pltpu.SemaphoreType.DMA((5,)),
            pltpu.SemaphoreType.DMA((8 + 4 * kv_heads,)),
            pltpu.SemaphoreType.DMA((8 + 4 * kv_heads,)),
        ],
        compiler_params=pltpu.CompilerParams(
            collective_id=0, has_side_effects=True, vmem_limit_bytes=56 * 1024 * 1024
        ),
        name="attend",
    )(queries, key_rows, value_rows, doc_lengths, block_owner)


def solution(mesh):
    rows = P(("seq", "ctx"), None)
    return jax.shard_map(
        functools.partial(body, mesh.shape["ctx"]),
        mesh=mesh,
        in_specs=(rows, rows, rows, P("seq"), P("seq")),
        out_specs=rows,
        check_vma=False,
    )
```

time: 22.8 us -> 21.6 us (0.947)
  Pallas kernels: 21.7 us -> 20.3 us
    pallas_call x1, Pallas kernels: 21.7 us -> 20.3 us  [body(): pl.pallas_call(functools.partial(kernel, devices), out_shape=pltpu.VMEM((...]
where the time goes in v1:
time: 21.6 us; the launch traced here: 21.3 us
  Pallas kernels  20.3 us (94%)
  local copies, waits for them, and re-layouts  0.97 us (4%)
    pallas_call x1, Pallas kernels, body(): pl.pallas_call(functools.partial(kernel, devices), out_shape=pltpu.VMEM((...  20.3 us
    unnamed x1, local copies, waits for them, and re-layouts  0.97 us

profile of v1, /device:TPU:28, one launch (start us, length us, event | category | flops | bytes accessed | tf_op | source)
XLA Modules:
  0.0 21.3 jit_solution(15374853770705882590)
XLA Ops:
  0.0 20.3 %attend.1 = bf16[256,2048]{1,0:T(8,128)(2,1)S(1)} custom-call(bf16[256,2048]{1,0:T(8,128)(2,1)} %q_hbm.1, bf16[256,512]{1,0:T(8,128)(2,1)} %k_hbm.1, bf16[256,512]{1,0:T(8,128)(2,1)} %v_hbm.1, s32[4]{0:T(128)} %lengths_hbm.1, s32[8]{0:T(128)} %owner_hbm.1), custom_call_target="tpu_custom_call" | custom-call | tf_op jit(solution)/shard_map/attend/pallas_call | solution.py:273
  20.4 1.0 %copy.7 = bf16[256,2048]{1,0:T(8,128)(2,1)} copy(bf16[256,2048]{1,0:T(8,128)(2,1)S(1)} %attend.1) | data formatting | bytes 2097152

commit v2 on v1

v2 whole, which is shorter than its diff:
```python
import functools
import itertools
import math

import jax
import jax.numpy as jnp
from jax import lax
from jax.experimental import pallas as pl
from jax.experimental.pallas import tpu as pltpu
from jax.sharding import PartitionSpec as P

HEAD_DIM = 128
BLOCK_ROWS = 128
GROUP_SIZE = 4
NEGATIVE = -1e30
MESH = pl.DeviceIdType.MESH
EXPONENT = HEAD_DIM ** -0.5 * math.log2(math.e)

OWN, PARTNER, PREV, CROSS = range(4)


def kernel(
    devices, q_hbm, k_hbm, v_hbm, lengths_hbm, owner_hbm, out,
    lengths, owner, q, kbuf, vbuf, bias, scores, top, weights, total, acc,
    q_far, k_far, v_far, far_bias, far_scores, far_weights, o_far,
    local_sem, send_sem, recv_sem, ready,
):
    rows = q.shape[0]
    kv_heads = kbuf.shape[2] // HEAD_DIM
    lent = kv_heads - 1
    half = rows // 2
    me = lax.axis_index("ctx")
    partner = me + 1 - 2 * (me % 2)
    prev = me - 2
    cross = partner - 2
    nxt = me + 2
    has_prev = me >= 2
    has_next = me < devices - 2
    no_prev = jnp.logical_not(has_prev)
    no_next = jnp.logical_not(has_next)
    whole = jnp.logical_or(has_next, no_prev)

    barrier = pltpu.get_barrier_semaphore()

    def greet(device):
        pl.semaphore_signal(barrier, inc=1, device_id={"ctx": device}, device_id_type=MESH)

    even = me % 2 == 0
    greet(partner)
    pl.when(jnp.logical_and(has_prev, even))(lambda: greet(prev))
    pl.when(has_next)(lambda: greet(nxt))

    local = [
        pltpu.make_async_copy(k_hbm, kbuf.at[OWN], local_sem.at[0]),
        pltpu.make_async_copy(v_hbm, vbuf.at[OWN], local_sem.at[1]),
        pltpu.make_async_copy(lengths_hbm, lengths, local_sem.at[2]),
        pltpu.make_async_copy(owner_hbm, owner, local_sem.at[3]),
        pltpu.make_async_copy(q_hbm, q, local_sem.at[4]),
    ]
    for copy in local:
        copy.start()
    below = jnp.logical_and(has_next, even).astype(jnp.int32)
    pl.semaphore_wait(barrier, 1 + has_prev.astype(jnp.int32) + below)

    @pl.when(jnp.logical_and(has_prev, jnp.logical_not(even)))
    def _():
        pl.semaphore_signal(ready, inc=1, device_id={"ctx": prev}, device_id_type=MESH)


    def column(head):
        return pl.ds(head * HEAD_DIM, HEAD_DIM)

    part = [pl.ds(0, half), pl.ds(half, half)]
    every = pl.ds(0, rows)
    rest = pl.ds(0, lent * HEAD_DIM)
    indices = itertools.count()

    def remote(source, target, device):
        index = next(indices)
        return pltpu.make_async_remote_copy(
            src_ref=source, dst_ref=target, send_sem=send_sem.at[index],
            recv_sem=recv_sem.at[index], device_id={"ctx": device}, device_id_type=MESH,
        )

    def own_copy(hbm, buf, piece, columns, chunk, device):
        return remote(hbm.at[piece, columns], buf.at[chunk, piece, columns], device)

    def relay(buf, chunk, piece, columns, device):
        return remote(buf.at[chunk, piece, columns], buf.at[CROSS, piece, columns], device)

    others = range(lent)
    straight = range(lent - 1)
    k_partner = [own_copy(k_hbm, kbuf, p, rest, PARTNER, partner) for p in part]
    k_next = [own_copy(k_hbm, kbuf, p, rest, PREV, nxt) for p in part]
    lent_partner = [
        own_copy(k_hbm, kbuf, every, column(lent), PARTNER, partner),
        own_copy(v_hbm, vbuf, every, column(lent), PARTNER, partner),
    ]
    v_first_partner = own_copy(v_hbm, vbuf, part[1], rest, PARTNER, partner)
    v_first_next = own_copy(v_hbm, vbuf, part[0], rest, PREV, nxt)
    v_partner = [own_copy(v_hbm, vbuf, part[0], column(g), PARTNER, partner) for g in others]
    v_next = [own_copy(v_hbm, vbuf, part[1], column(g), PREV, nxt) for g in others]
    k_to_next = [relay(kbuf, PARTNER, part[1], column(g), nxt) for g in straight]
    k_to_partner = [relay(kbuf, PREV, part[0], column(g), partner) for g in others]
    k_late = relay(kbuf, PREV, part[1], column(lent - 1), partner)
    v_to_partner = [relay(vbuf, PREV, part[0], column(g), partner) for g in others]
    v_late = [relay(vbuf, PREV, part[1], column(g), partner) for g in others]
    far_down = [
        remote(k_hbm.at[every, column(lent)], k_far.at[0], prev),
        remote(v_hbm.at[every, column(lent)], v_far.at[0], prev),
    ]
    far_across = [
        remote(k_far.at[0], k_far.at[1], partner),
        remote(v_far.at[0], v_far.at[1], partner),
    ]
    group = range(GROUP_SIZE)
    q_down = [
        remote(q_hbm.at[every, column(lent * GROUP_SIZE + j)], q_far.at[every, column(j)], prev)
        for j in group
    ]
    o_up = [
        remote(o_far.at[j], out.at[every, column(lent * GROUP_SIZE + j)], nxt) for j in group
    ]

    def start_all(copies):
        for copy in copies:
            copy.start()

    def receive_all(copies):
        for copy in copies:
            copy.wait_recv()

    def sent_all(copies):
        for copy in copies:
            copy.wait_send()

    k_partner[1].start()
    pl.when(whole)(lambda: start_all(lent_partner))
    pl.when(jnp.logical_and(has_next, jnp.logical_not(even)))(lambda: pl.semaphore_wait(ready, 1))

    @pl.when(has_next)
    def _():
        k_next[0].start()
        k_next[1].start()
        v_first_next.start()

    @pl.when(has_prev)
    def _():
        start_all(far_down)
        start_all(q_down)

    @pl.when(no_next)
    def _():
        k_partner[0].start()
        v_first_partner.start()

    local[2].wait()
    local[3].wait()
    down = lax.broadcasted_iota(jnp.int32, (half, 1), 0)
    along = lax.broadcasted_iota(jnp.int32, (1, half), 1)

    def mask(target, chunk, querier, device):
        for i in range(2):
            places = owner[2 * querier + i] * BLOCK_ROWS + down
            end = lengths[0]
            starts = jnp.where(places >= end, end, 0)
            for d in range(1, lengths.shape[0]):
                end = end + lengths[d]
                starts = jnp.where(places >= end, end, starts)
            for j in range(2):
                keys = owner[2 * device + j] * BLOCK_ROWS + along
                allowed = (keys >= starts) & (keys <= places)
                target[chunk, pl.ds(i * half, half), pl.ds(j * half, half)] = jnp.where(
                    allowed, 0.0, NEGATIVE
                )

    mask(bias, OWN, me, me)
    mask(bias, PARTNER, me, partner)

    @pl.when(has_prev)
    def _():
        mask(bias, PREV, me, prev)
        mask(bias, CROSS, me, cross)

    @pl.when(has_next)
    def _():
        mask(far_bias, 0, nxt, me)
        mask(far_bias, 1, nxt, partner)
        mask(far_bias, 2, nxt, nxt)
        mask(far_bias, 3, nxt, partner + 2)

    def attend(queries, keys, allowed):
        s = lax.dot_general(
            queries, keys, (((1,), (1,)), ((), ())), preferred_element_type=jnp.float32
        )
        return s + allowed

    def score(chunk, first, last):
        for g in range(first, last):
            keys = kbuf[chunk, :, column(g)]
            for j in group:
                h = g * GROUP_SIZE + j
                s = attend(q[:, column(h)], keys, bias[chunk])
                scores[h, chunk] = s
                best = jnp.maximum(s[:, :half], s[:, half:])
                if chunk != OWN:
                    best = jnp.maximum(best, top[h])
                top[h] = best

    def weigh(g, chunks):
        own = vbuf[OWN, :, column(g)]
        for j in group:
            h = g * GROUP_SIZE + j
            largest = jnp.max(top[h], axis=1, keepdims=True)
            summed = jnp.zeros((rows, half), jnp.float32)
            for c in range(chunks):
                w = jnp.exp2((scores[h, c] - largest) * EXPONENT)
                summed = summed + (w[:, :half] + w[:, half:])
                weights[h, c] = w.astype(jnp.bfloat16)
            total[h] = jnp.sum(summed, axis=1, keepdims=True)
            acc[h] = jnp.dot(weights[h, OWN], own, preferred_element_type=jnp.float32)

    def mix(g):
        partners = vbuf[PARTNER, :, column(g)]
        prevs = vbuf[PREV, :, column(g)]
        for j in group:
            h = g * GROUP_SIZE + j
            acc[h] += jnp.dot(
                weights[h, PARTNER], partners, preferred_element_type=jnp.float32
            ) + jnp.dot(weights[h, PREV], prevs, preferred_element_type=jnp.float32)

    def finish(chunk, g):
        values = vbuf[chunk, :, column(g)]
        for j in group:
            h = g * GROUP_SIZE + j
            mixed = acc[h] + jnp.dot(
                weights[h, chunk], values, preferred_element_type=jnp.float32
            )
            out[:, column(h)] = (mixed * (1.0 / total[h])).astype(jnp.bfloat16)

    def far_keys(c):
        return kbuf[c, :, column(lent)] if c < 2 else k_far[c - 2]

    def far_values(c):
        return vbuf[c, :, column(lent)] if c < 2 else v_far[c - 2]

    def far_score(j):
        q_down[j].wait_recv()
        for c in range(4):
            far_scores[j, c] = attend(q_far[:, column(j)], far_keys(c), far_bias[c])

    def far_finish(j):
        best = far_scores[j, 0]
        for c in range(1, 4):
            best = jnp.maximum(best, far_scores[j, c])
        largest = jnp.max(best, axis=1, keepdims=True)
        summed = jnp.zeros((rows, half), jnp.float32)
        for c in range(4):
            w = jnp.exp2((far_scores[j, c] - largest) * EXPONENT)
            summed = summed + (w[:, :half] + w[:, half:])
            far_weights[j, c] = w.astype(jnp.bfloat16)
        mixed = jnp.dot(far_weights[j, 0], far_values(0), preferred_element_type=jnp.float32)
        for c in range(1, 4):
            mixed += jnp.dot(far_weights[j, c], far_values(c), preferred_element_type=jnp.float32)
        share = 1.0 / jnp.sum(summed, axis=1, keepdims=True)
        o_far[j] = (mixed * share).astype(jnp.bfloat16)
        o_up[j].start()

    @pl.when(has_next)
    def _():
        for down_copy, across_copy in zip(far_down, far_across):
            down_copy.wait_recv()
            across_copy.start()
        k_partner[0].start()

    k_partner[1].wait_recv()

    @pl.when(has_next)
    def _():
        start_all(k_to_next)
        start_all(v_next)
        v_first_partner.start()

    @pl.when(has_prev)
    def _():
        k_next[0].wait_recv()
        start_all(k_to_partner)
        k_next[1].wait_recv()
        k_late.start()

    start_all(v_partner)
    local[0].wait()
    local[1].wait()
    local[4].wait()
    score(OWN, 0, lent)
    pl.when(no_prev)(lambda: score(OWN, lent, kv_heads))
    pl.when(whole)(lambda: receive_all(lent_partner))

    @pl.when(has_next)
    def _():
        far_across[0].wait_recv()
        far_score(0)
        far_score(1)
        far_across[1].wait_recv()
        far_finish(0)
        far_finish(1)
        for j in group[2:]:
            far_score(j)
            far_finish(j)

    k_partner[0].wait_recv()
    score(PARTNER, 0, lent)

    @pl.when(no_prev)
    def _():
        score(PARTNER, lent, kv_heads)
        for g in range(kv_heads):
            weigh(g, 2)
        v_first_partner.wait_recv()
        for g in range(kv_heads):
            if g < lent:
                v_partner[g].wait_recv()
            finish(PARTNER, g)

    @pl.when(has_prev)
    def _():
        score(PREV, 0, lent)
        for g in others:
            k_to_partner[g].wait_recv()
            (k_to_next[g] if g < lent - 1 else k_late).wait_recv()
            score(CROSS, g, g + 1)
            weigh(g, 4)
            if g == 1:
                v_first_next.wait_recv()
                start_all(v_to_partner)
        v_first_partner.wait_recv()
        for g in others:
            v_next[g].wait_recv()
            v_late[g].start()
            v_partner[g].wait_recv()
            mix(g)
        for g in others:
            v_to_partner[g].wait_recv()
            v_late[g].wait_recv()
            finish(CROSS, g)
        receive_all(o_up)

    sent_all(k_partner + v_partner + [v_first_partner])
    pl.when(whole)(lambda: sent_all(lent_partner))
    pl.when(has_next)(
        lambda: sent_all(k_next + k_to_next + v_next + far_across + o_up + [v_first_next])
    )
    pl.when(has_prev)(
        lambda: sent_all(k_to_partner + v_to_partner + v_late + far_down + q_down + [k_late])
    )


def body(devices, queries, key_rows, value_rows, doc_lengths, block_owner):
    rows, width = queries.shape
    kv_width = key_rows.shape[1]
    heads, kv_heads = width // HEAD_DIM, kv_width // HEAD_DIM
    half = rows // 2
    copies = 8 * kv_heads + 4 + 2 * GROUP_SIZE
    return pl.pallas_call(
        functools.partial(kernel, devices),
        out_shape=pltpu.VMEM((rows, width), jnp.bfloat16),
        in_specs=[pl.BlockSpec(memory_space=pl.ANY)] * 5,
        out_specs=pl.BlockSpec(memory_space=pltpu.VMEM),
        scratch_shapes=[
            pltpu.SMEM(doc_lengths.shape, jnp.int32),
            pltpu.SMEM(block_owner.shape, jnp.int32),
            pltpu.VMEM((rows, width), jnp.bfloat16),
            pltpu.VMEM((4, rows, kv_width), jnp.bfloat16),
            pltpu.VMEM((4, rows, kv_width), jnp.bfloat16),
            pltpu.VMEM((4, rows, rows), jnp.float32),
            pltpu.VMEM((heads, 4, rows, rows), jnp.float32),
            pltpu.VMEM((heads, rows, half), jnp.float32),
            pltpu.VMEM((heads, 4, rows, rows), jnp.bfloat16),
            pltpu.VMEM((heads, rows, 1), jnp.float32),
            pltpu.VMEM((heads, rows, HEAD_DIM), jnp.float32),
            pltpu.VMEM((rows, GROUP_SIZE * HEAD_DIM), jnp.bfloat16),
            pltpu.VMEM((2, rows, HEAD_DIM), jnp.bfloat16),
            pltpu.VMEM((2, rows, HEAD_DIM), jnp.bfloat16),
            pltpu.VMEM((4, rows, rows), jnp.float32),
            pltpu.VMEM((GROUP_SIZE, 4, rows, rows), jnp.float32),
            pltpu.VMEM((GROUP_SIZE, 4, rows, rows), jnp.bfloat16),
            pltpu.VMEM((GROUP_SIZE, rows, HEAD_DIM), jnp.bfloat16),
            pltpu.SemaphoreType.DMA((5,)),
            pltpu.SemaphoreType.DMA((copies,)),
            pltpu.SemaphoreType.DMA((copies,)),
            pltpu.SemaphoreType.REGULAR,
        ],
        compiler_params=pltpu.CompilerParams(
            collective_id=0, has_side_effects=True, vmem_limit_bytes=56 * 1024 * 1024
        ),
        name="attend",
    )(queries, key_rows, value_rows, doc_lengths, block_owner)


def solution(mesh):
    rows = P(("seq", "ctx"), None)
    return jax.shard_map(
        functools.partial(body, mesh.shape["ctx"]),
        mesh=mesh,
        in_specs=(rows, rows, rows, P("seq"), P("seq")),
        out_specs=rows,
        check_vma=False,
    )
```

time: 21.6 us -> 21.2 us (0.981)
    pallas_call x1, Pallas kernels: 20.3 us -> 20.1 us  [body(): pl.pallas_call(functools.partial(kernel, devices), out_shape=pltpu.VMEM((...]
where the time goes in v2:
time: 21.2 us; the launch traced here: 21.1 us
  Pallas kernels  20.1 us (95%)
  local copies, waits for them, and re-layouts  0.97 us (5%)
    pallas_call x1, Pallas kernels, body(): pl.pallas_call(functools.partial(kernel, devices), out_shape=pltpu.VMEM((...  20.1 us
    unnamed x1, local copies, waits for them, and re-layouts  0.97 us

profile of v2, /device:TPU:28, one launch (start us, length us, event | category | flops | bytes accessed | tf_op | source)
XLA Modules:
  0.0 21.1 jit_solution(8701954167279828386)
XLA Ops:
  0.0 20.1 %attend.1 = bf16[256,2048]{1,0:T(8,128)(2,1)S(1)} custom-call(bf16[256,2048]{1,0:T(8,128)(2,1)} %q_hbm.1, bf16[256,512]{1,0:T(8,128)(2,1)} %k_hbm.1, bf16[256,512]{1,0:T(8,128)(2,1)} %v_hbm.1, s32[4]{0:T(128)} %lengths_hbm.1, s32[8]{0:T(128)} %owner_hbm.1), custom_call_target="tpu_custom_call" | custom-call | tf_op jit(solution)/shard_map/attend/pallas_call | solution.py:364
  20.1 1.0 %copy.7 = bf16[256,2048]{1,0:T(8,128)(2,1)} copy(bf16[256,2048]{1,0:T(8,128)(2,1)S(1)} %attend.1) | data formatting | bytes 2097152

commit v3 on v2

--- a/solution.py
+++ b/solution.py
@@ -325,18 +325,19 @@
     @pl.when(has_prev)
     def _():
         score(PREV, 0, lent)
+        v_first_next.wait_recv()
+        start_all(v_to_partner)
         for g in others:
             k_to_partner[g].wait_recv()
             (k_to_next[g] if g < lent - 1 else k_late).wait_recv()
             score(CROSS, g, g + 1)
             weigh(g, 4)
-            if g == 1:
-                v_first_next.wait_recv()
-                start_all(v_to_partner)
+            if g == 0:
+                for value, late in zip(v_next, v_late):
+                    value.wait_recv()
+                    late.start()
         v_first_partner.wait_recv()
         for g in others:
-            v_next[g].wait_recv()
-            v_late[g].start()
             v_partner[g].wait_recv()
             mix(g)
         for g in others:

time: 21.2 us -> 20.8 us (0.981); the launches traced: 21.1 us -> 20.4 us
  Pallas kernels: 20.1 us -> 19.5 us
    pallas_call x1, Pallas kernels: 20.1 us -> 19.5 us  [body(): pl.pallas_call(functools.partial(kernel, devices), out_shape=pltpu.VMEM((...]
where the time goes in v3:
time: 20.8 us; the launch traced here: 20.4 us
  Pallas kernels  19.5 us (94%)
  local copies, waits for them, and re-layouts  0.97 us (5%)
    pallas_call x1, Pallas kernels, body(): pl.pallas_call(functools.partial(kernel, devices), out_shape=pltpu.VMEM((...  19.5 us
    unnamed x1, local copies, waits for them, and re-layouts  0.97 us

profile of v3, /device:TPU:28, one launch (start us, length us, event | category | flops | bytes accessed | tf_op | source)
XLA Modules:
  0.0 20.4 jit_solution(17111542879267704215)
XLA Ops:
  0.0 19.5 %attend.1 = bf16[256,2048]{1,0:T(8,128)(2,1)S(1)} custom-call(bf16[256,2048]{1,0:T(8,128)(2,1)} %q_hbm.1, bf16[256,512]{1,0:T(8,128)(2,1)} %k_hbm.1, bf16[256,512]{1,0:T(8,128)(2,1)} %v_hbm.1, s32[4]{0:T(128)} %lengths_hbm.1, s32[8]{0:T(128)} %owner_hbm.1), custom_call_target="tpu_custom_call" | custom-call | tf_op jit(solution)/shard_map/attend/pallas_call | solution.py:365
  19.5 1.0 %copy.7 = bf16[256,2048]{1,0:T(8,128)(2,1)} copy(bf16[256,2048]{1,0:T(8,128)(2,1)S(1)} %attend.1) | data formatting | bytes 2097152

commit v4 on v3

--- a/solution.py
+++ b/solution.py
@@ -98,7 +98,7 @@
     ]
     v_first_partner = own_copy(v_hbm, vbuf, part[1], rest, PARTNER, partner)
     v_first_next = own_copy(v_hbm, vbuf, part[0], rest, PREV, nxt)
-    v_partner = [own_copy(v_hbm, vbuf, part[0], column(g), PARTNER, partner) for g in others]
+    v_partner = [own_copy(v_hbm, vbuf, part[0], rest, PARTNER, partner)]
     v_next = [own_copy(v_hbm, vbuf, part[1], column(g), PREV, nxt) for g in others]
     k_to_next = [relay(kbuf, PARTNER, part[1], column(g), nxt) for g in straight]
     k_to_partner = [relay(kbuf, PREV, part[0], column(g), partner) for g in others]
@@ -318,8 +318,8 @@
             weigh(g, 2)
         v_first_partner.wait_recv()
         for g in range(kv_heads):
-            if g < lent:
-                v_partner[g].wait_recv()
+            if g == 0:
+                v_partner[0].wait_recv()
             finish(PARTNER, g)
 
     @pl.when(has_prev)
@@ -338,7 +338,8 @@
                     late.start()
         v_first_partner.wait_recv()
         for g in others:
-            v_partner[g].wait_recv()
+            if g == 0:
+                v_partner[0].wait_recv()
             mix(g)
         for g in others:
             v_to_partner[g].wait_recv()

time: 20.8 us -> 20.7 us (level)
  no operation moved by 1% of the time
where the time goes in v4:
time: 20.7 us; the launch traced here: 20.4 us
  Pallas kernels  19.5 us (94%)
  local copies, waits for them, and re-layouts  0.97 us (5%)
    pallas_call x1, Pallas kernels, body(): pl.pallas_call(functools.partial(kernel, devices), out_shape=pltpu.VMEM((...  19.5 us
    unnamed x1, local copies, waits for them, and re-layouts  0.97 us

profile of v4, /device:TPU:28, one launch (start us, length us, event | category | flops | bytes accessed | tf_op | source)
XLA Modules:
  0.0 20.4 jit_solution(7961256896728749174)
XLA Ops:
  0.0 19.5 %attend.1 = bf16[256,2048]{1,0:T(8,128)(2,1)S(1)} custom-call(bf16[256,2048]{1,0:T(8,128)(2,1)} %q_hbm.1, bf16[256,512]{1,0:T(8,128)(2,1)} %k_hbm.1, bf16[256,512]{1,0:T(8,128)(2,1)} %v_hbm.1, s32[4]{0:T(128)} %lengths_hbm.1, s32[8]{0:T(128)} %owner_hbm.1), custom_call_target="tpu_custom_call" | custom-call | tf_op jit(solution)/shard_map/attend/pallas_call | solution.py:366
  19.5 1.0 %copy.7 = bf16[256,2048]{1,0:T(8,128)(2,1)} copy(bf16[256,2048]{1,0:T(8,128)(2,1)S(1)} %attend.1) | data formatting | bytes 2097152

commit v5 on v4

--- a/solution.py
+++ b/solution.py
@@ -46,6 +46,8 @@
         pl.semaphore_signal(barrier, inc=1, device_id={"ctx": device}, device_id_type=MESH)
 
     even = me % 2 == 0
+    second = lax.axis_index("seq") % 2 == 1
+    first = jnp.logical_not(second)
     greet(partner)
     pl.when(jnp.logical_and(has_prev, even))(lambda: greet(prev))
     pl.when(has_next)(lambda: greet(nxt))
@@ -288,7 +290,7 @@
         k_next[1].wait_recv()
         k_late.start()
 
-    start_all(v_partner)
+    pl.when(first)(lambda: start_all(v_partner))
     local[0].wait()
     local[1].wait()
     local[4].wait()
@@ -310,6 +312,7 @@
 
     k_partner[0].wait_recv()
     score(PARTNER, 0, lent)
+    pl.when(second)(lambda: start_all(v_partner))
 
     @pl.when(no_prev)
     def _():

time: 20.7 us -> 20.6 us (level)
  no operation moved by 1% of the time
where the time goes in v5:
time: 20.6 us; the launch traced here: 20.4 us
  Pallas kernels  19.5 us (95%)
  local copies, waits for them, and re-layouts  0.97 us (5%)
    pallas_call x1, Pallas kernels, body(): pl.pallas_call(functools.partial(kernel, devices), out_shape=pltpu.VMEM((...  19.5 us
    unnamed x1, local copies, waits for them, and re-layouts  0.97 us

profile of v5, /device:TPU:28, one launch (start us, length us, event | category | flops | bytes accessed | tf_op | source)
XLA Modules:
  0.0 20.4 jit_solution(6309418749579097389)
XLA Ops:
  0.0 19.5 %attend.1 = bf16[256,2048]{1,0:T(8,128)(2,1)S(1)} custom-call(bf16[256,2048]{1,0:T(8,128)(2,1)} %q_hbm.1, bf16[256,512]{1,0:T(8,128)(2,1)} %k_hbm.1, bf16[256,512]{1,0:T(8,128)(2,1)} %v_hbm.1, s32[4]{0:T(128)} %lengths_hbm.1, s32[8]{0:T(128)} %owner_hbm.1), custom_call_target="tpu_custom_call" | custom-call | tf_op jit(solution)/shard_map/attend/pallas_call | solution.py:369
  19.5 1.0 %copy.7 = bf16[256,2048]{1,0:T(8,128)(2,1)} copy(bf16[256,2048]{1,0:T(8,128)(2,1)S(1)} %attend.1) | data formatting | bytes 2097152
